TPU v7x, 32 devices: a whole 2x2x4 slice. The times are simulated.
32 devices in a mesh: dp: 8 (over y, x, core), tensor: 4 (over z).
Axes of the slice: x: 2, y: 2, z: 4, core: 2. Of those that a mesh axis runs over, the one named last changes fastest.
Arguments:
- hidden_in: bfloat16 [8, 128, 16384], P('dp'), may hold values from -6 to 6
- value_weight: bfloat16 [16384, 256], P(None, 'tensor'), may hold values from -0.046875 to 0.046875
- queries: bfloat16 [8, 128, 4096], P('dp', None, 'tensor'), may hold values from -4 to 4
- key_rows: bfloat16 [8, 128, 256], P('dp', None, 'tensor'), may hold values from -4 to 4
- attention_out: bfloat16 [8, 128, 4096], P('dp', None, 'tensor'), may hold values from -4 to 4
- output_grad: bfloat16 [8, 128, 4096], P('dp', None, 'tensor'), may hold values from -6 to 6
- log_normalizer: float32 [8, 128, 32], P('dp', None, 'tensor'), may hold values from 1 to 5
- document_ids: int32 [8, 128], P('dp'), may hold values from 0 to 3, never falling along the last dimension, each value on 1 to 64 neighbouring positions
Outputs:
- query_grad: bfloat16 [8, 128, 4096], P('dp', None, 'tensor')
- key_grad: bfloat16 [8, 128, 256], P('dp', None, 'tensor')
- input_grad: bfloat16 [8, 128, 16384], P('dp', 'tensor')
- value_weight_grad: float32 [16384, 256], P('dp', 'tensor')
Inputs may be any that keep to these rules, and one draw needn't show every extreme that they name: `document_ids`: within one group the ids never fall; all 4 documents occur, each of 1 to 64 tokens.
All inputs are finite; a program needn't handle non-finite values.
Results may differ from a plain program's by a relative error of at most 0.014.
Values may be sent and summed in bfloat16 or wider, within the bound.
A program may use at most 64 MiB of HBM per device.

v0:
```python
import math

import jax
import jax.numpy as jnp
from jax import lax
from jax.sharding import PartitionSpec as P


def partner(value, axis, distance):
    mask = 2**distance
    pairs = [(source, source ^ mask) for source in range(lax.axis_size(axis))]
    return lax.ppermute(value, axis, pairs)


def per_device(
    hidden_in,
    value_weight,
    queries,
    key_rows,
    attention_out,
    output_grad,
    log_normalizer,
    document_ids,
):
    tokens = hidden_in.shape[1]
    head_count = log_normalizer.shape[2]
    half_width = key_rows.shape[2]
    head_width = 2 * half_width
    score_scale = 1.0 / math.sqrt(head_width)
    inputs_local = hidden_in[0]
    value_half = jnp.dot(inputs_local, value_weight, preferred_element_type=jnp.float32).astype(
        jnp.bfloat16
    )
    key_half = key_rows[0]
    other_key, other_value = partner((key_half, value_half), "tensor", 0)
    pair_member = lax.axis_index("tensor") % 2
    lower_member = pair_member == 0
    keys_full = jnp.where(
        lower_member,
        jnp.concatenate([key_half, other_key], 1),
        jnp.concatenate([other_key, key_half], 1),
    )
    values_full = jnp.where(
        lower_member,
        jnp.concatenate([value_half, other_value], 1),
        jnp.concatenate([other_value, value_half], 1),
    )
    query_heads = queries[0].reshape(tokens, head_count, head_width)
    grad_heads = output_grad[0].reshape(tokens, head_count, head_width)
    out_heads = attention_out[0].reshape(tokens, head_count, head_width)
    position = jnp.arange(tokens, dtype=jnp.int32)
    documents = document_ids[0]
    allowed = (position[None, :] <= position[:, None]) & (documents[:, None] == documents[None, :])
    scores = (
        jnp.einsum("thd,sd->hts", query_heads, keys_full, preferred_element_type=jnp.float32)
        * score_scale
    )
    normalizers = jnp.transpose(log_normalizer[0])[:, :, None]
    probabilities = jnp.where(allowed[None], jnp.exp(scores - normalizers), 0.0)
    probs_low = probabilities.astype(jnp.bfloat16)
    value_part = jnp.einsum(
        "hts,thd->sd", probs_low, grad_heads, preferred_element_type=jnp.float32
    )
    row_dots = jnp.einsum("thd,thd->ht", grad_heads, out_heads, preferred_element_type=jnp.float32)
    prob_grad = jnp.einsum(
        "thd,sd->hts", grad_heads, values_full, preferred_element_type=jnp.float32
    )
    score_grad = (probabilities * (prob_grad - row_dots[:, :, None]) * score_scale).astype(
        jnp.bfloat16
    )
    query_grad = jnp.einsum(
        "hts,sd->thd", score_grad, keys_full, preferred_element_type=jnp.float32
    )
    query_grad = query_grad.astype(jnp.bfloat16).reshape(1, tokens, head_count * head_width)
    key_part = jnp.einsum(
        "hts,thd->sd", score_grad, query_heads, preferred_element_type=jnp.float32
    )
    own_offset = pair_member * half_width
    other_offset = (1 - pair_member) * half_width
    send_key = lax.dynamic_slice_in_dim(key_part, other_offset, half_width, 1)
    send_value = lax.dynamic_slice_in_dim(value_part, other_offset, half_width, 1)
    got_key, got_value = partner((send_key, send_value), "tensor", 0)
    key_sum = lax.dynamic_slice_in_dim(key_part, own_offset, half_width, 1) + got_key
    value_sum = lax.dynamic_slice_in_dim(value_part, own_offset, half_width, 1) + got_value
    key_grad = key_sum.astype(jnp.bfloat16).reshape(1, tokens, half_width)
    value_grad = value_sum.astype(jnp.bfloat16)
    input_sum = lax.psum_scatter(
        lax.dot_general(
            value_grad, value_weight, (((1,), (1,)), ((), ())), preferred_element_type=jnp.float32
        ).astype(jnp.bfloat16),
        "tensor",
        scatter_dimension=0,
        tiled=True,
    ).astype(jnp.float32)
    weight_grad = lax.psum_scatter(
        lax.dot_general(
            inputs_local, value_grad, (((0,), (0,)), ((), ())), preferred_element_type=jnp.float32
        ),
        "dp",
        scatter_dimension=0,
        tiled=True,
    )
    input_grad = input_sum.astype(jnp.bfloat16).reshape((1,) + input_sum.shape)
    return (query_grad, key_grad, input_grad, weight_grad)


def solution(mesh):
    return jax.shard_map(
        per_device,
        mesh=mesh,
        in_specs=(
            P("dp", None, None),
            P(None, "tensor"),
            P("dp", None, "tensor"),
            P("dp", None, "tensor"),
            P("dp", None, "tensor"),
            P("dp", None, "tensor"),
            P("dp", None, "tensor"),
            P("dp", None),
        ),
        out_specs=(
            P("dp", None, "tensor"),
            P("dp", None, "tensor"),
            P("dp", "tensor", None),
            P("dp", "tensor"),
        ),
        check_vma=False,
    )
```

profile of v0, /device:TPU:0, one launch (start us, length us, event | category | flops | bytes accessed | tf_op | source)
XLA Modules:
  0.0 161.9 jit_solution(10721417009186592288)
XLA Ops:
  7.2 0.0 copy-start
  7.2 0.0 reduce-scatter.5.cloned.1.call-start
  7.2 3.1 %collective-permute-start = (bf16[128,64]{0,1:T(8,128)(2,1)}, bf16[128,64]{0,1:T(8,128)(2,1)S(1)}, u32[]{:S(2)}, u32[]{:S(2)}) collective-permute-start(bf16[128,64]{0,1:T(8,128)(2,1)} %bitcast.79), channel_id=1, source_target_pairs={{0,1},{1,0},{2,3},{3,2},{4,5},{5,4},{6,7},{7,6},{8,9},{9,8},{10,11... | collective-permute-start | bytes 49160 | tf_op jit(solution)/shard_map/ppermute | solution.py:12
  10.3 0.8 fusion.16
  11.2 1.1 copy.37
  12.3 1.0 copy.38
  13.3 0.2 copy.20
  13.5 0.0 collective-permute-done
  13.6 1.1 fusion.7
  14.6 0.2 convolution_bitcast_fusion.2
  14.9 0.8 collective-permute-start.3
  15.7 3.2 %collective-permute-done.3 = f32[128,64]{0,1:T(8,128)S(1)} collective-permute-done((f32[128,64]{0,1:T(8,128)S(1)}, f32[128,64]{0,1:T(8,128)S(1)}, u32[]{:S(2)}, u32[]{:S(2)}) %collective-permute-start.3) | collective-permute-done | bytes 32800 | tf_op jit(solution)/shard_map/ppermute | solution.py:12
  18.9 4.9 %convolution_bitcast_fusion = f32[16384,64]{0,1:T(8,128)} fusion(bf16[128,64]{0,1:T(8,128)(2,1)S(1)} %add_convert_fusion, bf16[1,128,16384]{2,1,0:T(8,128)(2,1)} %param.8), kind=kOutput, calls=%fused_computation.1 | convolution fusion | flops 268435456 | bytes 8404992 | tf_op jit(solution)/shard_map/dot_general | solution.py:96
  23.8 0.0 reduce-scatter.5.cloned.1.call-update
  23.8 0.0 reduce-scatter.3.cloned.1.call-start
  23.8 3.2 %convolution_convert_fusion = bf16[128,16384]{1,0:T(8,128)(2,1)} fusion(bf16[128,64]{0,1:T(8,128)(2,1)S(1)} %add_convert_fusion, bf16[16384,64]{0,1:T(8,128)(2,1)S(1)} %copy-done), kind=kOutput, calls=%fused_computation | convolution fusion | flops 270532608 | bytes 6307840 | tf_op jit(solution)/shard_map/dot_general | solution.py:88
  27.0 0.0 reduce-scatter.3.cloned.1.call-update
  27.1 0.0 copy-start.1
  27.1 0.0 copy-start.2
  27.1 3.8 %fusion.11 = bf16[128,64]{0,1:T(8,128)(2,1)S(1)} fusion(bf16[16384,64]{0,1:T(8,128)(2,1)S(1)} %copy-done, bf16[1,128,16384]{2,1,0:T(8,128)(2,1)} %param.8), kind=kOutput, calls=%fused_computation.18 | convolution fusion | flops 268443648 | bytes 6307840 | tf_op jit(solution)/shard_map/dot_general | solution.py:31
  30.9 0.8 collective-permute-start.1
  31.7 0.2 fusion.14
  32.0 2.7 %collective-permute-done.1 = bf16[128,64]{0,1:T(8,128)(2,1)S(1)} collective-permute-done((bf16[128,64]{0,1:T(8,128)(2,1)S(1)}, bf16[128,64]{0,1:T(8,128)(2,1)S(1)}, u32[]{:S(2)}, u32[]{:S(2)}) %collective-permute-start.1) | collective-permute-done | bytes 16416 | tf_op jit(solution)/shard_map/ppermute | solution.py:12
  34.7 0.3 fusion.10
  35.0 0.2 convolution_bitcast_fusion.3
  35.2 0.8 collective-permute-start.2
  36.0 0.2 convolution_convert_fusion.1
  36.2 0.9 copy.21
  37.1 2.1 %collective-permute-done.2 = f32[128,64]{0,1:T(8,128)S(1)} collective-permute-done((f32[128,64]{0,1:T(8,128)S(1)}, f32[128,64]{0,1:T(8,128)S(1)}, u32[]{:S(2)}, u32[]{:S(2)}) %collective-permute-start.2) | collective-permute-done | bytes 32800 | tf_op jit(solution)/shard_map/ppermute | solution.py:12
  39.2 0.6 fusion.28
  39.8 35.6 %reduce-scatter.5.cloned.1.call-done = f32[2048,64]{0,1:T(8,128)} async-done(((f32[16384,64]{0,1:T(8,128)}), f32[2048,64]{0,1:T(8,128)}) %reduce-scatter.5.cloned.1.call-update) | async-done | bytes 524304 | tf_op jit(solution)/shard_map/reduce_scatter | solution.py:95
  75.4 79.7 %reduce-scatter.3.cloned.1.call-done = bf16[32,16384]{1,0:T(8,128)(2,1)} async-done(((bf16[128,16384]{1,0:T(8,128)(2,1)}), bf16[32,16384]{1,0:T(8,128)(2,1)}) %reduce-scatter.3.cloned.1.call-update) | async-done | bytes 1048592 | tf_op jit(solution)/shard_map/reduce_scatter | solution.py:87
  (8 shorter events, 0.1 us)
Async XLA Ops:
  7.2 16.7 %copy-start = (bf16[16384,64]{0,1:T(8,128)(2,1)S(1)}, bf16[16384,64]{0,1:T(8,128)(2,1)}, u32[]{:S(2)}) copy-start(bf16[16384,64]{0,1:T(8,128)(2,1)} %param.9) | copy-start | bytes 6291460
  7.2 68.3 %reduce-scatter.5.cloned.1.call-start = ((), (), s32[]{:S(2)}) async-start(), calls=%async_computation.3 | async-start | bytes 4718592 | tf_op jit(solution)/shard_map/reduce_scatter | solution.py:95
  7.2 6.3 %collective-permute-start = (bf16[128,64]{0,1:T(8,128)(2,1)}, bf16[128,64]{0,1:T(8,128)(2,1)S(1)}, u32[]{:S(2)}, u32[]{:S(2)}) collective-permute-start(bf16[128,64]{0,1:T(8,128)(2,1)} %bitcast.79), channel_id=1, source_target_pairs={{0,1},{1,0},{2,3},{3,2},{4,5},{5,4},{6,7},{7,6},{8,9},{9,8},{10,11... | collective-permute-start | bytes 49160 | tf_op jit(solution)/shard_map/ppermute | solution.py:12
  14.9 4.0 %collective-permute-start.3 = (f32[128,64]{0,1:T(8,128)S(1)}, f32[128,64]{0,1:T(8,128)S(1)}, u32[]{:S(2)}, u32[]{:S(2)}) collective-permute-start(f32[128,64]{0,1:T(8,128)S(1)} %constant_dynamic-slice_fusion), channel_id=1, source_target_pairs={{0,1},{1,0},{2,3},{3,2},{4,5},{5,4},{6,7},{7,6},{8,9},{9,8},{10,11... | collective-permute-start | bytes 98312 | tf_op jit(solution)/shard_map/ppermute | solution.py:12
  23.8 131.3 %reduce-scatter.3.cloned.1.call-start = ((), (), s32[]{:S(2)}) async-start(), calls=%async_computation.2 | async-start | bytes 5242880 | tf_op jit(solution)/shard_map/reduce_scatter | solution.py:87
  27.1 4.6 %copy-start.1 = (bf16[1,128,1024]{2,1,0:T(8,128)(2,1)S(1)}, bf16[1,128,1024]{2,1,0:T(8,128)(2,1)}, u32[]{:S(2)}) copy-start(bf16[1,128,1024]{2,1,0:T(8,128)(2,1)} %param.12) | copy-start | bytes 786436
  27.1 8.9 %copy-start.2 = (bf16[1,128,64]{1,2,0:T(8,128)(2,1)S(1)}, bf16[1,128,64]{1,2,0:T(8,128)(2,1)}, u32[]{:S(2)}) copy-start(bf16[1,128,64]{1,2,0:T(8,128)(2,1)} %param.11) | copy-start | bytes 49156
  30.9 3.8 %collective-permute-start.1 = (bf16[128,64]{0,1:T(8,128)(2,1)S(1)}, bf16[128,64]{0,1:T(8,128)(2,1)S(1)}, u32[]{:S(2)}, u32[]{:S(2)}) collective-permute-start(bf16[128,64]{0,1:T(8,128)(2,1)S(1)} %fusion.11), channel_id=1, source_target_pairs={{0,1},{1,0},{2,3},{3,2},{4,5},{5,4},{6,7},{7,6},{8,9},{9,8},{10,11... | collective-permute-start | bytes 49160 | tf_op jit(solution)/shard_map/ppermute | solution.py:12
  35.2 4.0 %collective-permute-start.2 = (f32[128,64]{0,1:T(8,128)S(1)}, f32[128,64]{0,1:T(8,128)S(1)}, u32[]{:S(2)}, u32[]{:S(2)}) collective-permute-start(f32[128,64]{0,1:T(8,128)S(1)} %constant_dynamic-slice_fusion.1), channel_id=1, source_target_pairs={{0,1},{1,0},{2,3},{3,2},{4,5},{5,4},{6,7},{7,6},{8,9},{9,8},{10,11... | collective-permute-start | bytes 98312 | tf_op jit(solution)/shard_map/ppermute | solution.py:12
Sparse Core Ops, SparseCore 0:
  23.9 51.4 reduce-scatter.4
  78.3 76.7 reduce-scatter.2
where the time goes:
time: 162 us
  waiting for transfers between devices  123 us (76%)
  between operations  14.2 us (9%)
  matrix products  13.9 us (9%)
  starting transfers between devices  5.57 us (3%)
  local copies, waits for them, and re-layouts  3.33 us (2%)
  other arithmetic  1.65 us (1%)
    reduce_scatter x1, waiting for transfers between devices, per_device(): lax.psum_scatter(lax.dot_general(value_grad, value_weight, (((1,), (1,)),...  79.7 us
    reduce_scatter x1, waiting for transfers between devices, per_device(): lax.psum_scatter(lax.dot_general(inputs_local, value_grad, (((0,), (0,)),...  35.6 us
    ppermute x4, waiting for transfers between devices, partner(): return lax.ppermute(value, axis, pairs)  7.99 us
    ppermute x4, starting transfers between devices, partner(): return lax.ppermute(value, axis, pairs)  5.49 us
    dot_general x1, matrix products, per_device(): lax.dot_general(inputs_local, value_grad, (((0,), (0,)), ((), ())), prefe...  4.86 us
    dot_general x1, matrix products, per_device(): jnp.dot(inputs_local, value_weight, preferred_element_type=jnp.float32)  3.79 us
  transfers between devices with their start and end apart: 6, of which 5 were waited for; matrix products, arithmetic and copies ran while one was open for 8% of the time, Pallas kernels for 0%

commit v1 on v0

--- a/solution.py
+++ b/solution.py
@@ -1,9 +1,334 @@
+import functools
 import math
 
 import jax
 import jax.numpy as jnp
 from jax import lax
+from jax.experimental import pallas as pl
+from jax.experimental.pallas import tpu as pltpu
 from jax.sharding import PartitionSpec as P
+
+MESH = pl.DeviceIdType.MESH
+F32 = jnp.float32
+BF16 = jnp.bfloat16
+NT = (((1,), (1,)), ((), ()))
+
+
+def fused(
+    groups,
+    ranks,
+    hidden_hbm,
+    weight_hbm,
+    queries_ref,
+    key_ref,
+    out_ref,
+    grad_ref,
+    norm_ref,
+    doc_ref,
+    qg_ref,
+    kg_ref,
+    ig_ref,
+    wg_ref,
+    hidden,
+    weight,
+    piece,
+    keys_t,
+    values_t,
+    probs,
+    part,
+    got_part,
+    grads_t,
+    out_buf,
+    core_send,
+    core_got,
+    chip_send,
+    chip_got,
+    load_sem,
+    pair_send,
+    pair_recv,
+    wa_send,
+    wa_recv,
+    wb_send,
+    wb_recv,
+    vg_send,
+    vg_recv,
+    dc_send,
+    dc_recv,
+    dx_send,
+    dx_recv,
+    o_send,
+    o_recv,
+):
+    d = lax.axis_index("dp")
+    t = lax.axis_index("tensor")
+    member = t % 2
+    pair = t + 1 - 2 * member
+    core = d % 2
+    chip = d // 2
+    other_core = d + 1 - 2 * core
+    chips = groups // 2
+    tokens, width = hidden.shape
+    half = weight.shape[0]
+    heads = norm_ref.shape[0]
+    hd = 2 * half
+    scale = 1.0 / math.sqrt(hd)
+    span = width // ranks
+    sub = span // groups
+    rows = tokens // ranks
+    wg_cols = width // groups
+
+    def ds(index, size):
+        return pl.ds(pl.multiple_of(index * size, size), size)
+
+    def remote(src, dst, send, recv, **device):
+        return pltpu.make_async_remote_copy(
+            src_ref=src, dst_ref=dst, send_sem=send, recv_sem=recv,
+            device_id=device, device_id_type=MESH,
+        )
+
+    started = []
+
+    def send(src, dst, ssem, rsem, **device):
+        copy = remote(src, dst, ssem, rsem, **device)
+        copy.start()
+        started.append(copy)
+
+    load_w = pltpu.make_async_copy(weight_hbm, weight, load_sem.at[0])
+    load_h = pltpu.make_async_copy(hidden_hbm, hidden, load_sem.at[1])
+    load_p = pltpu.make_async_copy(
+        weight_hbm.at[:, ds(t, span)], piece.at[ds(t, half), :], load_sem.at[2]
+    )
+    load_p.start()
+    load_h.start()
+    load_w.start()
+    load_k = pltpu.make_async_copy(key_ref, keys_t.at[member], load_sem.at[3])
+    load_k.start()
+
+    barrier = pltpu.get_barrier_semaphore()
+    for r in range(1, ranks):
+        pl.semaphore_signal(barrier, inc=1, device_id={"tensor": (t + r) % ranks}, device_id_type=MESH)
+    for i in range(1, groups):
+        pl.semaphore_signal(barrier, inc=1, device_id={"dp": (d + i) % groups}, device_id_type=MESH)
+    pl.semaphore_wait(barrier, ranks + groups - 2)
+
+    send(key_ref, keys_t.at[member], pair_send.at[0], pair_recv.at[0], tensor=pair)
+    for r in range(1, ranks):
+        to = (t + r) % ranks
+        send(
+            weight_hbm.at[:, ds(to * groups + d, sub)],
+            piece.at[ds(t, half), ds(d, sub)],
+            wa_send.at[to], wa_recv.at[t], tensor=to,
+        )
+
+    lane = lax.broadcasted_iota(jnp.int32, (tokens, hd), 1)
+    dots = jnp.zeros((tokens, hd), F32)
+    for j in range(heads):
+        cols = slice(j * hd, (j + 1) * hd)
+        product = grad_ref[:, cols].astype(F32) * out_ref[:, cols].astype(F32)
+        dots = jnp.where(lane == j, jnp.sum(product, axis=1, keepdims=True), dots)
+    dots = dots.T
+    doc_row = jnp.broadcast_to(doc_ref[...].astype(F32), (tokens, tokens))
+    doc_col = doc_row.T
+    s_index = lax.broadcasted_iota(jnp.int32, (tokens, tokens), 0)
+    t_index = lax.broadcasted_iota(jnp.int32, (tokens, tokens), 1)
+    allowed = (s_index <= t_index) & (doc_row == doc_col)
+
+    load_k.wait()
+    remote(key_ref, keys_t.at[1 - member], pair_send.at[0], pair_recv.at[0], tensor=pair).wait_recv()
+    keys = keys_t[...].reshape(hd, tokens).astype(F32).T.astype(BF16)
+    total = jnp.zeros((tokens, hd), F32)
+    for j in range(heads):
+        cols = slice(j * hd, (j + 1) * hd)
+        scores = lax.dot_general(keys, queries_ref[:, cols], NT, preferred_element_type=F32) * scale
+        prob = jnp.where(allowed, jnp.exp(scores - norm_ref[j : j + 1, :]), 0.0)
+        probs[j] = prob
+        total += jnp.dot(prob.astype(BF16), grad_ref[:, cols], preferred_element_type=F32)
+    part[0] = total.T
+    send(
+        part.at[0, ds(1 - member, half), :], got_part.at[0],
+        pair_send.at[1], pair_recv.at[1], tensor=pair,
+    )
+
+    for r in range(1, ranks):
+        source = (t + r) % ranks
+        block = piece.at[ds(source, half), ds(d, sub)]
+        remote(block, block, wa_send.at[source], wa_recv.at[source], tensor=source).wait_recv()
+        for i in range(1, groups):
+            to = (d + i) % groups
+            send(block, block, wb_send.at[source, to], wb_recv.at[source, d], dp=to)
+
+    load_w.wait()
+    load_h.wait()
+    chunk = wg_cols
+    value = jnp.zeros((half, tokens), F32)
+    for c in range(width // chunk):
+        cols = slice(c * chunk, (c + 1) * chunk)
+        value += lax.dot_general(weight[:, cols], hidden[:, cols], NT, preferred_element_type=F32)
+    values_t[member] = value.astype(BF16)
+    send(values_t.at[member], values_t.at[member], pair_send.at[2], pair_recv.at[2], tensor=pair)
+
+    remote(got_part.at[0], got_part.at[0], pair_send.at[1], pair_recv.at[1], tensor=pair).wait_recv()
+    grad_own = (part[0, ds(member, half), :] + got_part[0]).astype(BF16)
+    grads_t[ds(t, half), :] = grad_own
+    for r in range(1, ranks):
+        to = (t + r) % ranks
+        block = grads_t.at[ds(t, half), :]
+        send(block, block, vg_send.at[to], vg_recv.at[t], tensor=to)
+
+    def partial_wg(owner):
+        return jnp.dot(grad_own, hidden[:, ds(owner, wg_cols)], preferred_element_type=F32)
+
+    for i in range(chips):
+        c = (chip + 1 + i) % chips
+        core_send[i] = partial_wg(c * 2 + 1 - core).astype(BF16)
+        send(core_send.at[i], core_got.at[i], dc_send.at[i], dc_recv.at[i], dp=other_core)
+
+    for r in range(1, ranks):
+        source = (t + r) % ranks
+        block = grads_t.at[ds(source, half), :]
+        remote(block, block, vg_send.at[source], vg_recv.at[source], tensor=source).wait_recv()
+    grads = grads_t[...].astype(F32).T.astype(BF16)
+    load_p.wait()
+
+    def input_chunk(i):
+        g = (d + groups - i) % groups
+        if i:
+            for r in range(1, ranks):
+                source = (t + r) % ranks
+                block = piece.at[ds(source, half), ds(g, sub)]
+                remote(block, block, wb_send.at[source, g], wb_recv.at[source, g], dp=g).wait_recv()
+        out_buf[i] = jnp.dot(grads, piece[:, ds(g, sub)], preferred_element_type=F32).astype(BF16)
+        place = ds(t * groups + g, sub)
+        for r in range(1, ranks):
+            to = (t + r) % ranks
+            send(
+                out_buf.at[i, ds(to, rows), :], ig_ref.at[:, place],
+                o_send.at[to, g], o_recv.at[t, g], tensor=to,
+            )
+        ig_ref[:, place] = out_buf[i, ds(t, rows), :]
+
+    input_chunk(0)
+
+    for i in range(chips):
+        remote(core_send.at[i], core_got.at[i], dc_send.at[i], dc_recv.at[i], dp=other_core).wait_recv()
+        if i < chips - 1:
+            c = (chip + 1 + i) % chips
+            chip_send[i] = (partial_wg(c * 2 + core) + core_got[i].astype(F32)).astype(BF16)
+            send(chip_send.at[i], chip_got.at[i], dx_send.at[i], dx_recv.at[i], dp=c * 2 + core)
+    wg_ref[...] = partial_wg(d) + core_got[chips - 1].astype(F32)
+
+    input_chunk(1)
+    input_chunk(2)
+
+    remote(values_t.at[1 - member], values_t.at[1 - member], pair_send.at[2], pair_recv.at[2], tensor=pair).wait_recv()
+    values = values_t[...].reshape(hd, tokens).astype(F32).T.astype(BF16)
+    total = jnp.zeros((tokens, hd), F32)
+    for j in range(heads):
+        cols = slice(j * hd, (j + 1) * hd)
+        prob_grad = lax.dot_general(values, grad_ref[:, cols], NT, preferred_element_type=F32)
+        score_grad = probs[j] * (prob_grad - dots[j : j + 1, :]) * scale
+        total += jnp.dot(score_grad.astype(BF16), queries_ref[:, cols], preferred_element_type=F32)
+        qg_ref[:, cols] = jnp.dot(
+            score_grad.T.astype(BF16), keys, preferred_element_type=F32
+        ).astype(BF16)
+    part[1] = total.T
+    send(
+        part.at[1, ds(1 - member, half), :], got_part.at[1],
+        pair_send.at[3], pair_recv.at[3], tensor=pair,
+    )
+
+    for i in range(3, groups):
+        input_chunk(i)
+
+    remote(got_part.at[1], got_part.at[1], pair_send.at[3], pair_recv.at[3], tensor=pair).wait_recv()
+    kg_ref[...] = (part[1, ds(member, half), :] + got_part[1]).astype(BF16)
+
+    for i in range(chips - 1):
+        c = (chip + chips - 1 - i) % chips
+        remote(chip_send.at[i], chip_got.at[i], dx_send.at[i], dx_recv.at[i], dp=c * 2 + core).wait_recv()
+        wg_ref[...] += chip_got[i].astype(F32)
+
+    for r in range(1, ranks):
+        source = (t + r) % ranks
+        for i in range(groups):
+            g = (d + groups - i) % groups
+            place = ig_ref.at[:, ds(source * groups + g, sub)]
+            remote(
+                out_buf.at[0, ds(source, rows), :], place,
+                o_send.at[source, g], o_recv.at[source, g], tensor=source,
+            ).wait_recv()
+    for copy in started:
+        copy.wait_send()
+
+
+def fused_per_device(groups, ranks, hidden_in, value_weight, queries, key_rows, attention_out,
+                     output_grad, log_normalizer, document_ids):
+    _, tokens, width = hidden_in.shape
+    half = value_weight.shape[1]
+    hd = 2 * half
+    heads = log_normalizer.shape[2]
+    span = width // ranks
+    sub = span // groups
+    chips = groups // 2
+    wg_cols = width // groups
+    vmem = pl.BlockSpec(memory_space=pltpu.VMEM)
+    hbm = pl.BlockSpec(memory_space=pl.ANY)
+    sem = pltpu.SemaphoreType.DMA
+    query_grad, key_grad, input_grad, weight_grad = pl.pallas_call(
+        functools.partial(fused, groups, ranks),
+        out_shape=(
+            jax.ShapeDtypeStruct((tokens, heads * hd), BF16),
+            jax.ShapeDtypeStruct((half, tokens), BF16),
+            jax.ShapeDtypeStruct((tokens // ranks, width), BF16),
+            jax.ShapeDtypeStruct((half, wg_cols), F32),
+        ),
+        in_specs=[hbm, hbm] + [vmem] * 6,
+        out_specs=(vmem,) * 4,
+        scratch_shapes=[
+            pltpu.VMEM((tokens, width), BF16),
+            pltpu.VMEM((half, width), BF16),
+            pltpu.VMEM((ranks * half, span), BF16),
+            pltpu.VMEM((2, half, tokens), BF16),
+            pltpu.VMEM((2, half, tokens), BF16),
+            pltpu.VMEM((heads, tokens, tokens), F32),
+            pltpu.VMEM((2, hd, tokens), F32),
+            pltpu.VMEM((2, half, tokens), F32),
+            pltpu.VMEM((ranks * half, tokens), BF16),
+            pltpu.VMEM((groups, tokens, sub), BF16),
+            pltpu.VMEM((chips, half, wg_cols), BF16),
+            pltpu.VMEM((chips, half, wg_cols), BF16),
+            pltpu.VMEM((chips - 1, half, wg_cols), BF16),
+            pltpu.VMEM((chips - 1, half, wg_cols), BF16),
+            sem((4,)),
+            sem((4,)),
+            sem((4,)),
+            sem((ranks,)),
+            sem((ranks,)),
+            sem((ranks, groups)),
+            sem((ranks, groups)),
+            sem((ranks,)),
+            sem((ranks,)),
+            sem((chips,)),
+            sem((chips,)),
+            sem((chips,)),
+            sem((chips,)),
+            sem((ranks, groups)),
+            sem((ranks, groups)),
+        ],
+        compiler_params=pltpu.CompilerParams(
+            collective_id=0, has_side_effects=True, vmem_limit_bytes=40 * 1024 * 1024
+        ),
+    )(
+        hidden_in[0],
+        value_weight.T,
+        queries[0],
+        key_rows[0].T,
+        attention_out[0],
+        output_grad[0],
+        log_normalizer[0].T,
+        document_ids,
+    )
+    return query_grad[None], key_grad.T[None], input_grad[None], weight_grad.T
 
 
 def partner(value, axis, distance):
@@ -105,8 +430,16 @@
 
 
 def solution(mesh):
+    groups, ranks = mesh.shape["dp"], mesh.shape["tensor"]
+
+    def body(*operands):
+        width = operands[0].shape[2]
+        if width % (groups * ranks * 128) == 0:
+            return fused_per_device(groups, ranks, *operands)
+        return per_device(*operands)
+
     return jax.shard_map(
-        per_device,
+        body,
         mesh=mesh,
         in_specs=(
             P("dp", None, None),

time: 162 us -> 61.3 us (0.38)
  waiting for transfers between devices: 123 us -> 0 us
  Pallas kernels: 0 us -> 48.6 us
  matrix products: 13.9 us -> 0 us
  between operations: 14.2 us -> 0.66 us
  local copies, waits for them, and re-layouts: 3.33 us -> 11.8 us
  starting transfers between devices: 5.57 us -> 0 us
  other arithmetic: 1.65 us -> 0 us
    reduce_scatter x2 -> x0, waiting for transfers between devices: 115 us -> none  [the longest x1 79.7 us: per_device(): lax.psum_scatter(lax.dot_general(value_grad, value_weight, (((1,), (1,)),...]
    pallas_call x0 -> x1, Pallas kernels: none -> 48.6 us  [fused_per_device(): pl.pallas_call(functools.partial(fused, groups, ranks), out_shape=(jax.Sh...]
    dot_general x8 -> x0, matrix products: 13.9 us -> none  [the longest x1 4.86 us: per_device(): lax.dot_general(inputs_local, value_grad, (((0,), (0,)), ((), ())), prefe...]
    unnamed x9 -> x20, local copies, waits for them, and re-layouts: 1.91 us -> 11.8 us
    ppermute x4 -> x0, waiting for transfers between devices: 7.99 us -> none  [partner(): return lax.ppermute(value, axis, pairs)]
    ppermute x4 -> x0, starting transfers between devices: 5.49 us -> none  [partner(): return lax.ppermute(value, axis, pairs)]
  transfers between devices with their start and end apart: 6 -> 0, of which waited for: 5 -> 0; matrix products, arithmetic and copies ran while one was open for 8% -> 0% of each run, Pallas kernels for 0% -> 0%
where the time goes in v1:
time: 61.3 us; the launch traced here: 61 us
  Pallas kernels  48.6 us (79%)
  local copies, waits for them, and re-layouts  11.8 us (19%)
  between operations  0.66 us (1%)
    pallas_call x1, Pallas kernels, fused_per_device(): pl.pallas_call(functools.partial(fused, groups, ranks), out_shape=(jax.Sh...  48.6 us
    unnamed x20, local copies, waits for them, and re-layouts  11.8 us

profile of v1, /device:TPU:0, one launch (start us, length us, event | category | flops | bytes accessed | tf_op | source)
XLA Modules:
  0.0 61.0 jit_solution(12218521637555101679)
XLA Ops:
  0.6 0.0 copy-start
  0.6 2.2 %copy-done = bf16[1,128,16384]{2,1,0:T(8,128)(2,1)S(1)} copy-done((bf16[1,128,16384]{2,1,0:T(8,128)(2,1)S(1)}, bf16[1,128,16384]{2,1,0:T(8,128)(2,1)}, u32[]{:S(2)}) %copy-start) | copy-done | bytes 4194328
  2.8 0.0 copy-start.1
  2.8 1.6 %copy-done.1 = bf16[16384,64]{0,1:T(8,128)(2,1)S(1)} copy-done((bf16[16384,64]{0,1:T(8,128)(2,1)S(1)}, bf16[16384,64]{0,1:T(8,128)(2,1)}, u32[]{:S(2)}) %copy-start.1) | copy-done | bytes 2097176
  4.4 0.0 copy-start.2
  4.4 0.9 %copy-done.2 = bf16[1,128,1024]{2,1,0:T(8,128)(2,1)S(1)} copy-done((bf16[1,128,1024]{2,1,0:T(8,128)(2,1)S(1)}, bf16[1,128,1024]{2,1,0:T(8,128)(2,1)}, u32[]{:S(2)}) %copy-start.2) | copy-done | bytes 262168
  5.4 0.0 copy-start.3
  5.4 0.9 %copy-done.3 = bf16[1,128,1024]{2,1,0:T(8,128)(2,1)S(1)} copy-done((bf16[1,128,1024]{2,1,0:T(8,128)(2,1)S(1)}, bf16[1,128,1024]{2,1,0:T(8,128)(2,1)}, u32[]{:S(2)}) %copy-start.3) | copy-done | bytes 262168
  6.3 0.0 copy-start.4
  6.3 0.9 %copy-done.4 = bf16[1,128,1024]{2,1,0:T(8,128)(2,1)S(1)} copy-done((bf16[1,128,1024]{2,1,0:T(8,128)(2,1)S(1)}, bf16[1,128,1024]{2,1,0:T(8,128)(2,1)}, u32[]{:S(2)}) %copy-start.4) | copy-done | bytes 262168
  7.3 0.0 copy-start.5
  7.3 0.7 %copy-done.5 = bf16[1,128,64]{1,2,0:T(8,128)(2,1)S(1)} copy-done((bf16[1,128,64]{1,2,0:T(8,128)(2,1)S(1)}, bf16[1,128,64]{1,2,0:T(8,128)(2,1)}, u32[]{:S(2)}) %copy-start.5) | copy-done | bytes 16408
  8.0 0.0 copy-start.6
  8.0 0.7 %copy-done.6 = f32[1,128,8]{1,2,0:T(8,128)S(1)} copy-done((f32[1,128,8]{1,2,0:T(8,128)S(1)}, f32[1,128,8]{1,2,0:T(8,128)}, u32[]{:S(2)}) %copy-start.6) | copy-done | bytes 4120
  8.7 0.0 copy-start.7
  8.7 0.7 %copy-done.7 = s32[1,128]{1,0:T(1,128)S(1)} copy-done((s32[1,128]{1,0:T(1,128)S(1)}, s32[1,128]{1,0:T(1,128)}, u32[]{:S(2)}) %copy-start.7) | copy-done | bytes 536
  9.3 48.6 %shard_map.111 = (bf16[128,1024]{1,0:T(8,128)(2,1)S(1)}, bf16[64,128]{1,0:T(8,128)(2,1)S(1)}, bf16[32,16384]{1,0:T(8,128)(2,1)S(1)}, f32[64,2048]{1,0:T(8,128)S(1)}) custom-call(bf16[128,16384]{1,0:T(8,128)(2,1)S(1)} %bitcast.17, bf16[64,16384]{1,0:T(8,128)(2,1)S(1)} %bitcast.18, bf16[128,1024]{1,0:T(8,128)(2,1)S(1)} %bitcast.21, ...), custom_call_target="tpu_custom_call" | custom-call | tf_op jit(solution)/shard_map/pallas_call | solution.py:277
  57.9 0.7 %copy.16 = bf16[1,128,1024]{2,1,0:T(8,128)(2,1)} copy(bf16[1,128,1024]{2,1,0:T(8,128)(2,1)S(1)} %bitcast.24) | data formatting | bytes 524288
  58.6 0.6 copy.17
  59.2 1.0 %copy.18 = bf16[1,32,16384]{2,1,0:T(8,128)(2,1)} copy(bf16[1,32,16384]{2,1,0:T(8,128)(2,1)S(1)} %bitcast.19) | data formatting | bytes 2097152
  60.2 0.8 %copy.19 = f32[2048,64]{0,1:T(8,128)} copy(f32[2048,64]{0,1:T(8,128)S(1)} %bitcast.20) | data formatting | bytes 1048576
Async XLA Ops:
  0.6 2.2 %copy-start = (bf16[1,128,16384]{2,1,0:T(8,128)(2,1)S(1)}, bf16[1,128,16384]{2,1,0:T(8,128)(2,1)}, u32[]{:S(2)}) copy-start(bf16[1,128,16384]{2,1,0:T(8,128)(2,1)} %param.8) | copy-start | bytes 12582916
  2.8 1.6 %copy-start.1 = (bf16[16384,64]{0,1:T(8,128)(2,1)S(1)}, bf16[16384,64]{0,1:T(8,128)(2,1)}, u32[]{:S(2)}) copy-start(bf16[16384,64]{0,1:T(8,128)(2,1)} %param.9) | copy-start | bytes 6291460
  4.4 0.9 %copy-start.2 = (bf16[1,128,1024]{2,1,0:T(8,128)(2,1)S(1)}, bf16[1,128,1024]{2,1,0:T(8,128)(2,1)}, u32[]{:S(2)}) copy-start(bf16[1,128,1024]{2,1,0:T(8,128)(2,1)} %param.10) | copy-start | bytes 786436
  5.4 0.9 %copy-start.3 = (bf16[1,128,1024]{2,1,0:T(8,128)(2,1)S(1)}, bf16[1,128,1024]{2,1,0:T(8,128)(2,1)}, u32[]{:S(2)}) copy-start(bf16[1,128,1024]{2,1,0:T(8,128)(2,1)} %param.12) | copy-start | bytes 786436
  6.3 0.9 %copy-start.4 = (bf16[1,128,1024]{2,1,0:T(8,128)(2,1)S(1)}, bf16[1,128,1024]{2,1,0:T(8,128)(2,1)}, u32[]{:S(2)}) copy-start(bf16[1,128,1024]{2,1,0:T(8,128)(2,1)} %param.13) | copy-start | bytes 786436
  7.3 0.7 %copy-start.5 = (bf16[1,128,64]{1,2,0:T(8,128)(2,1)S(1)}, bf16[1,128,64]{1,2,0:T(8,128)(2,1)}, u32[]{:S(2)}) copy-start(bf16[1,128,64]{1,2,0:T(8,128)(2,1)} %param.11) | copy-start | bytes 49156
  8.0 0.7 %copy-start.6 = (f32[1,128,8]{1,2,0:T(8,128)S(1)}, f32[1,128,8]{1,2,0:T(8,128)}, u32[]{:S(2)}) copy-start(f32[1,128,8]{1,2,0:T(8,128)} %param.14) | copy-start | bytes 12292
  8.7 0.7 %copy-start.7 = (s32[1,128]{1,0:T(1,128)S(1)}, s32[1,128]{1,0:T(1,128)}, u32[]{:S(2)}) copy-start(s32[1,128]{1,0:T(1,128)} %doc_ref.1) | copy-start | bytes 1540

commit v2 on v1

--- a/solution.py
+++ b/solution.py
@@ -19,18 +19,23 @@
     ranks,
     hidden_hbm,
     weight_hbm,
-    queries_ref,
+    queries_hbm,
     key_ref,
-    out_ref,
-    grad_ref,
-    norm_ref,
-    doc_ref,
+    out_hbm,
+    grad_hbm,
+    norm_hbm,
+    doc_hbm,
     qg_ref,
     kg_ref,
     ig_ref,
     wg_ref,
     hidden,
     weight,
+    queries_ref,
+    out_ref,
+    grad_ref,
+    norm_ref,
+    doc_ref,
     piece,
     keys_t,
     values_t,
@@ -50,6 +55,7 @@
     wa_recv,
     wb_send,
     wb_recv,
+    fw_send,
     vg_send,
     vg_recv,
     dc_send,
@@ -98,11 +104,14 @@
     load_p = pltpu.make_async_copy(
         weight_hbm.at[:, ds(t, span)], piece.at[ds(t, half), :], load_sem.at[2]
     )
-    load_p.start()
-    load_h.start()
-    load_w.start()
     load_k = pltpu.make_async_copy(key_ref, keys_t.at[member], load_sem.at[3])
-    load_k.start()
+    load_g = pltpu.make_async_copy(grad_hbm, grad_ref, load_sem.at[4])
+    load_o = pltpu.make_async_copy(out_hbm, out_ref, load_sem.at[5])
+    load_q = pltpu.make_async_copy(queries_hbm, queries_ref, load_sem.at[6])
+    load_n = pltpu.make_async_copy(norm_hbm, norm_ref, load_sem.at[7])
+    load_d = pltpu.make_async_copy(doc_hbm, doc_ref, load_sem.at[8])
+    for load in (load_k, load_d, load_n, load_g, load_o, load_q, load_w, load_h, load_p):
+        load.start()
 
     barrier = pltpu.get_barrier_semaphore()
     for r in range(1, ranks):
@@ -120,6 +129,9 @@
             wa_send.at[to], wa_recv.at[t], tensor=to,
         )
 
+    load_g.wait()
+    load_o.wait()
+    load_d.wait()
     lane = lax.broadcasted_iota(jnp.int32, (tokens, hd), 1)
     dots = jnp.zeros((tokens, hd), F32)
     for j in range(heads):
@@ -134,6 +146,8 @@
     allowed = (s_index <= t_index) & (doc_row == doc_col)
 
     load_k.wait()
+    load_q.wait()
+    load_n.wait()
     remote(key_ref, keys_t.at[1 - member], pair_send.at[0], pair_recv.at[0], tensor=pair).wait_recv()
     keys = keys_t[...].reshape(hd, tokens).astype(F32).T.astype(BF16)
     total = jnp.zeros((tokens, hd), F32)
@@ -153,8 +167,7 @@
         source = (t + r) % ranks
         block = piece.at[ds(source, half), ds(d, sub)]
         remote(block, block, wa_send.at[source], wa_recv.at[source], tensor=source).wait_recv()
-        for i in range(1, groups):
-            to = (d + i) % groups
+        for to in [other_core] + [(chip + i) % chips * 2 + core for i in range(1, chips)]:
             send(block, block, wb_send.at[source, to], wb_recv.at[source, d], dp=to)
 
     load_w.wait()
@@ -190,13 +203,27 @@
     grads = grads_t[...].astype(F32).T.astype(BF16)
     load_p.wait()
 
+    order = [d, other_core]
+    straight = [(chip + chips - i) % chips * 2 + core for i in range(1, chips)]
+    for i in range(chips - 1):
+        order.append(straight[i])
+        if i:
+            order.append(straight[i - 1] + 1 - 2 * core)
+    order.append(straight[-1] + 1 - 2 * core)
+
+    def arrive(i):
+        g = order[i]
+        for r in range(1, ranks):
+            source = (t + r) % ranks
+            block = piece.at[ds(source, half), ds(g, sub)]
+            remote(block, block, wb_send.at[source, g], wb_recv.at[source, g], dp=other_core).wait_recv()
+            if any(g is s for s in straight):
+                send(block, block, fw_send.at[source, g], wb_recv.at[source, g], dp=other_core)
+
     def input_chunk(i):
-        g = (d + groups - i) % groups
+        g = order[i]
         if i:
-            for r in range(1, ranks):
-                source = (t + r) % ranks
-                block = piece.at[ds(source, half), ds(g, sub)]
-                remote(block, block, wb_send.at[source, g], wb_recv.at[source, g], dp=g).wait_recv()
+            arrive(i)
         out_buf[i] = jnp.dot(grads, piece[:, ds(g, sub)], preferred_element_type=F32).astype(BF16)
         place = ds(t * groups + g, sub)
         for r in range(1, ranks):
@@ -261,6 +288,18 @@
         copy.wait_send()
 
 
+def write_out(*refs):
+    count = len(refs) // 2
+    sems = refs[-1]
+    copies = [
+        pltpu.make_async_copy(refs[i], refs[count + i], sems.at[i]) for i in range(count)
+    ]
+    for copy in copies:
+        copy.start()
+    for copy in copies:
+        copy.wait()
+
+
 def fused_per_device(groups, ranks, hidden_in, value_weight, queries, key_rows, attention_out,
                      output_grad, log_normalizer, document_ids):
     _, tokens, width = hidden_in.shape
@@ -272,7 +311,7 @@
     chips = groups // 2
     wg_cols = width // groups
     vmem = pl.BlockSpec(memory_space=pltpu.VMEM)
-    hbm = pl.BlockSpec(memory_space=pl.ANY)
+    hbm = pl.BlockSpec(memory_space=pltpu.HBM)
     sem = pltpu.SemaphoreType.DMA
     query_grad, key_grad, input_grad, weight_grad = pl.pallas_call(
         functools.partial(fused, groups, ranks),
@@ -282,11 +321,16 @@
             jax.ShapeDtypeStruct((tokens // ranks, width), BF16),
             jax.ShapeDtypeStruct((half, wg_cols), F32),
         ),
-        in_specs=[hbm, hbm] + [vmem] * 6,
+        in_specs=[hbm] * 8,
         out_specs=(vmem,) * 4,
         scratch_shapes=[
             pltpu.VMEM((tokens, width), BF16),
             pltpu.VMEM((half, width), BF16),
+            pltpu.VMEM((tokens, heads * hd), BF16),
+            pltpu.VMEM((tokens, heads * hd), BF16),
+            pltpu.VMEM((tokens, heads * hd), BF16),
+            pltpu.VMEM((heads, tokens), F32),
+            pltpu.VMEM((1, tokens), jnp.int32),
             pltpu.VMEM((ranks * half, span), BF16),
             pltpu.VMEM((2, half, tokens), BF16),
             pltpu.VMEM((2, half, tokens), BF16),
@@ -299,11 +343,12 @@
             pltpu.VMEM((chips, half, wg_cols), BF16),
             pltpu.VMEM((chips - 1, half, wg_cols), BF16),
             pltpu.VMEM((chips - 1, half, wg_cols), BF16),
-            sem((4,)),
+            sem((9,)),
             sem((4,)),
             sem((4,)),
             sem((ranks,)),
             sem((ranks,)),
+            sem((ranks, groups)),
             sem((ranks, groups)),
             sem((ranks, groups)),
             sem((ranks,)),
@@ -316,7 +361,7 @@
             sem((ranks, groups)),
         ],
         compiler_params=pltpu.CompilerParams(
-            collective_id=0, has_side_effects=True, vmem_limit_bytes=40 * 1024 * 1024
+            collective_id=0, has_side_effects=True, vmem_limit_bytes=56 * 1024 * 1024
         ),
     )(
         hidden_in[0],
@@ -328,6 +373,14 @@
         log_normalizer[0].T,
         document_ids,
     )
+    results = (query_grad, key_grad, input_grad, weight_grad)
+    query_grad, key_grad, input_grad, weight_grad = pl.pallas_call(
+        write_out,
+        out_shape=tuple(jax.ShapeDtypeStruct(x.shape, x.dtype) for x in results),
+        in_specs=[vmem] * len(results),
+        out_specs=(hbm,) * len(results),
+        scratch_shapes=[sem((len(results),))],
+    )(*results)
     return query_grad[None], key_grad.T[None], input_grad[None], weight_grad.T
 
 

time: 61.3 us -> 48.9 us (0.80)
  local copies, waits for them, and re-layouts: 11.8 us -> 0 us
    unnamed x20 -> x0, local copies, waits for them, and re-layouts: 11.8 us -> none
    pallas_call x1, Pallas kernels: 48.6 us -> 45.4 us  [fused_per_device(): pl.pallas_call(functools.partial(fused, groups, ranks), out_shape=(jax.Sh...]
    pallas_call x0 -> x1, Pallas kernels: none -> 2.72 us  [fused_per_device(): pl.pallas_call(write_out, out_shape=tuple((jax.ShapeDtypeStruct(x.shape,...]
where the time goes in v2:
time: 48.9 us; the launch traced here: 48.7 us
  Pallas kernels  48.1 us (98%)
  between operations  0.64 us (1%)
    pallas_call x1, Pallas kernels, fused_per_device(): pl.pallas_call(functools.partial(fused, groups, ranks), out_shape=(jax.Sh...  45.4 us
    pallas_call x1, Pallas kernels, fused_per_device(): pl.pallas_call(write_out, out_shape=tuple((jax.ShapeDtypeStruct(x.shape,...  2.72 us

profile of v2, /device:TPU:0, one launch (start us, length us, event | category | flops | bytes accessed | tf_op | source)
XLA Modules:
  0.0 48.7 jit_solution(15479626066733343445)
XLA Ops:
  0.6 45.4 %shard_map.111 = (bf16[128,1024]{1,0:T(8,128)(2,1)}, bf16[64,128]{1,0:T(8,128)(2,1)}, bf16[32,16384]{1,0:T(8,128)(2,1)}, f32[64,2048]{1,0:T(8,128)}) custom-call(bf16[128,16384]{1,0:T(8,128)(2,1)} %bitcast.17, bf16[64,16384]{1,0:T(8,128)(2,1)} %bitcast.18, bf16[128,1024]{1,0:T(8,128)(2,1)} %bitcast.19, bf16[64,128]{1,0:T(8,128)(2,1)} %bitcast.22, ...), custom_call_target="tpu_custom_call" | custom-call | tf_op jit(solution)/shard_map/pallas_call | solution.py:316
  46.0 2.7 %shard_map.112 = (bf16[128,1024]{1,0:T(8,128)(2,1)}, bf16[64,128]{1,0:T(8,128)(2,1)}, bf16[32,16384]{1,0:T(8,128)(2,1)}, f32[64,2048]{1,0:T(8,128)}) custom-call(bf16[128,1024]{1,0:T(8,128)(2,1)} %get-tuple-element.12.refs_0_, bf16[64,128]{1,0:T(8,128)(2,1)} %get-tuple-element.13.refs_1_, bf16[32,16384]{1,0:T(8,128)(2,1)} %get-tuple-element.14.refs_2_, ...), custom_call_target="tpu_custom_call" | custom-call | tf_op jit(solution)/shard_map/pallas_call | solution.py:377

commit v3 on v2

--- a/solution.py
+++ b/solution.py
@@ -43,6 +43,7 @@
     part,
     got_part,
     grads_t,
+    grads_ref,
     out_buf,
     core_send,
     core_got,
@@ -78,7 +79,7 @@
     heads = norm_ref.shape[0]
     hd = 2 * half
     scale = 1.0 / math.sqrt(hd)
-    span = width // ranks
+    span = width // 2
     sub = span // groups
     rows = tokens // ranks
     wg_cols = width // groups
@@ -102,7 +103,7 @@
     load_w = pltpu.make_async_copy(weight_hbm, weight, load_sem.at[0])
     load_h = pltpu.make_async_copy(hidden_hbm, hidden, load_sem.at[1])
     load_p = pltpu.make_async_copy(
-        weight_hbm.at[:, ds(t, span)], piece.at[ds(t, half), :], load_sem.at[2]
+        weight_hbm.at[:, ds(member, span)], piece.at[ds(t, half), :], load_sem.at[2]
     )
     load_k = pltpu.make_async_copy(key_ref, keys_t.at[member], load_sem.at[3])
     load_g = pltpu.make_async_copy(grad_hbm, grad_ref, load_sem.at[4])
@@ -124,7 +125,7 @@
     for r in range(1, ranks):
         to = (t + r) % ranks
         send(
-            weight_hbm.at[:, ds(to * groups + d, sub)],
+            weight_hbm.at[:, ds(to % 2 * groups + d, sub)],
             piece.at[ds(t, half), ds(d, sub)],
             wa_send.at[to], wa_recv.at[t], tensor=to,
         )
@@ -200,7 +201,8 @@
         source = (t + r) % ranks
         block = grads_t.at[ds(source, half), :]
         remote(block, block, vg_send.at[source], vg_recv.at[source], tensor=source).wait_recv()
-    grads = grads_t[...].astype(F32).T.astype(BF16)
+    grads_ref[...] = grads_t[...].astype(F32).T.astype(BF16)
+    grads = grads_ref[ds(t // 2, 2 * rows), :]
     load_p.wait()
 
     order = [d, other_core]
@@ -225,14 +227,12 @@
         if i:
             arrive(i)
         out_buf[i] = jnp.dot(grads, piece[:, ds(g, sub)], preferred_element_type=F32).astype(BF16)
-        place = ds(t * groups + g, sub)
-        for r in range(1, ranks):
-            to = (t + r) % ranks
-            send(
-                out_buf.at[i, ds(to, rows), :], ig_ref.at[:, place],
-                o_send.at[to, g], o_recv.at[t, g], tensor=to,
-            )
-        ig_ref[:, place] = out_buf[i, ds(t, rows), :]
+        place = ds(member * groups + g, sub)
+        send(
+            out_buf.at[i, ds(1 - member, rows), :], ig_ref.at[:, place],
+            o_send.at[g], o_recv.at[g], tensor=pair,
+        )
+        ig_ref[:, place] = out_buf[i, ds(member, rows), :]
 
     input_chunk(0)
 
@@ -275,15 +275,11 @@
         remote(chip_send.at[i], chip_got.at[i], dx_send.at[i], dx_recv.at[i], dp=c * 2 + core).wait_recv()
         wg_ref[...] += chip_got[i].astype(F32)
 
-    for r in range(1, ranks):
-        source = (t + r) % ranks
-        for i in range(groups):
-            g = (d + groups - i) % groups
-            place = ig_ref.at[:, ds(source * groups + g, sub)]
-            remote(
-                out_buf.at[0, ds(source, rows), :], place,
-                o_send.at[source, g], o_recv.at[source, g], tensor=source,
-            ).wait_recv()
+    for g in order:
+        place = ig_ref.at[:, ds((1 - member) * groups + g, sub)]
+        remote(
+            out_buf.at[0, ds(member, rows), :], place, o_send.at[g], o_recv.at[g], tensor=pair
+        ).wait_recv()
     for copy in started:
         copy.wait_send()
 
@@ -306,7 +302,7 @@
     half = value_weight.shape[1]
     hd = 2 * half
     heads = log_normalizer.shape[2]
-    span = width // ranks
+    span = width // 2
     sub = span // groups
     chips = groups // 2
     wg_cols = width // groups
@@ -338,7 +334,8 @@
             pltpu.VMEM((2, hd, tokens), F32),
             pltpu.VMEM((2, half, tokens), F32),
             pltpu.VMEM((ranks * half, tokens), BF16),
-            pltpu.VMEM((groups, tokens, sub), BF16),
+            pltpu.VMEM((tokens, ranks * half), BF16),
+            pltpu.VMEM((groups, 2 * (tokens // ranks), sub), BF16),
             pltpu.VMEM((chips, half, wg_cols), BF16),
             pltpu.VMEM((chips, half, wg_cols), BF16),
             pltpu.VMEM((chips - 1, half, wg_cols), BF16),
@@ -357,8 +354,8 @@
             sem((chips,)),
             sem((chips,)),
             sem((chips,)),
-            sem((ranks, groups)),
-            sem((ranks, groups)),
+            sem((groups,)),
+            sem((groups,)),
         ],
         compiler_params=pltpu.CompilerParams(
             collective_id=0, has_side_effects=True, vmem_limit_bytes=56 * 1024 * 1024
@@ -487,7 +484,7 @@
 
     def body(*operands):
         width = operands[0].shape[2]
-        if width % (groups * ranks * 128) == 0:
+        if width % (groups * ranks * 128) == 0 and ranks % 2 == 0:
             return fused_per_device(groups, ranks, *operands)
         return per_device(*operands)
 

time: 48.9 us -> 55 us (1.12)
  Pallas kernels: 48.1 us -> 54.2 us
    pallas_call x1, Pallas kernels: 45.4 us -> 51.5 us  [fused_per_device(): pl.pallas_call(functools.partial(fused, groups, ranks), out_shape=(jax.Sh...]
where the time goes in v3:
time: 55 us; the launch traced here: 54.9 us
  Pallas kernels  54.2 us (99%)
  between operations  0.64 us (1%)
    pallas_call x1, Pallas kernels, fused_per_device(): pl.pallas_call(functools.partial(fused, groups, ranks), out_shape=(jax.Sh...  51.5 us
    pallas_call x1, Pallas kernels, fused_per_device(): pl.pallas_call(write_out, out_shape=tuple((jax.ShapeDtypeStruct(x.shape,...  2.72 us

profile of v3, /device:TPU:0, one launch (start us, length us, event | category | flops | bytes accessed | tf_op | source)
XLA Modules:
  0.0 54.9 jit_solution(5229486791062531120)
XLA Ops:
  0.6 51.5 %shard_map.111 = (bf16[128,1024]{1,0:T(8,128)(2,1)}, bf16[64,128]{1,0:T(8,128)(2,1)}, bf16[32,16384]{1,0:T(8,128)(2,1)}, f32[64,2048]{1,0:T(8,128)}) custom-call(bf16[128,16384]{1,0:T(8,128)(2,1)} %bitcast.17, bf16[64,16384]{1,0:T(8,128)(2,1)} %bitcast.18, bf16[128,1024]{1,0:T(8,128)(2,1)} %bitcast.19, bf16[64,128]{1,0:T(8,128)(2,1)} %bitcast.22, ...), custom_call_target="tpu_custom_call" | custom-call | tf_op jit(solution)/shard_map/pallas_call | solution.py:312
  52.1 2.7 %shard_map.112 = (bf16[128,1024]{1,0:T(8,128)(2,1)}, bf16[64,128]{1,0:T(8,128)(2,1)}, bf16[32,16384]{1,0:T(8,128)(2,1)}, f32[64,2048]{1,0:T(8,128)}) custom-call(bf16[128,1024]{1,0:T(8,128)(2,1)} %get-tuple-element.12.refs_0_, bf16[64,128]{1,0:T(8,128)(2,1)} %get-tuple-element.13.refs_1_, bf16[32,16384]{1,0:T(8,128)(2,1)} %get-tuple-element.14.refs_2_, ...), custom_call_target="tpu_custom_call" | custom-call | tf_op jit(solution)/shard_map/pallas_call | solution.py:374

commit v4 on v2

--- a/solution.py
+++ b/solution.py
@@ -244,8 +244,9 @@
             send(chip_send.at[i], chip_got.at[i], dx_send.at[i], dx_recv.at[i], dp=c * 2 + core)
     wg_ref[...] = partial_wg(d) + core_got[chips - 1].astype(F32)
 
-    input_chunk(1)
-    input_chunk(2)
+    early = groups - 2
+    for i in range(1, early):
+        input_chunk(i)
 
     remote(values_t.at[1 - member], values_t.at[1 - member], pair_send.at[2], pair_recv.at[2], tensor=pair).wait_recv()
     values = values_t[...].reshape(hd, tokens).astype(F32).T.astype(BF16)
@@ -264,7 +265,7 @@
         pair_send.at[3], pair_recv.at[3], tensor=pair,
     )
 
-    for i in range(3, groups):
+    for i in range(early, groups):
         input_chunk(i)
 
     remote(got_part.at[1], got_part.at[1], pair_send.at[3], pair_recv.at[3], tensor=pair).wait_recv()

time: 48.9 us -> 48.9 us (level)
  no operation moved by 1% of the time
where the time goes in v4:
time: 48.9 us; the launch traced here: 48.7 us
  Pallas kernels  48.1 us (98%)
  between operations  0.64 us (1%)
    pallas_call x1, Pallas kernels, fused_per_device(): pl.pallas_call(functools.partial(fused, groups, ranks), out_shape=(jax.Sh...  45.4 us
    pallas_call x1, Pallas kernels, fused_per_device(): pl.pallas_call(write_out, out_shape=tuple((jax.ShapeDtypeStruct(x.shape,...  2.72 us

profile of v4, /device:TPU:0, one launch (start us, length us, event | category | flops | bytes accessed | tf_op | source)
XLA Modules:
  0.0 48.7 jit_solution(1495932077178355978)
XLA Ops:
  0.6 45.4 %shard_map.111 = (bf16[128,1024]{1,0:T(8,128)(2,1)}, bf16[64,128]{1,0:T(8,128)(2,1)}, bf16[32,16384]{1,0:T(8,128)(2,1)}, f32[64,2048]{1,0:T(8,128)}) custom-call(bf16[128,16384]{1,0:T(8,128)(2,1)} %bitcast.17, bf16[64,16384]{1,0:T(8,128)(2,1)} %bitcast.18, bf16[128,1024]{1,0:T(8,128)(2,1)} %bitcast.19, bf16[64,128]{1,0:T(8,128)(2,1)} %bitcast.22, ...), custom_call_target="tpu_custom_call" | custom-call | tf_op jit(solution)/shard_map/pallas_call | solution.py:317
  46.0 2.7 %shard_map.112 = (bf16[128,1024]{1,0:T(8,128)(2,1)}, bf16[64,128]{1,0:T(8,128)(2,1)}, bf16[32,16384]{1,0:T(8,128)(2,1)}, f32[64,2048]{1,0:T(8,128)}) custom-call(bf16[128,1024]{1,0:T(8,128)(2,1)} %get-tuple-element.12.refs_0_, bf16[64,128]{1,0:T(8,128)(2,1)} %get-tuple-element.13.refs_1_, bf16[32,16384]{1,0:T(8,128)(2,1)} %get-tuple-element.14.refs_2_, ...), custom_call_target="tpu_custom_call" | custom-call | tf_op jit(solution)/shard_map/pallas_call | solution.py:378
